TPU v7x, 128 devices: a whole 4x4x4 slice. The times are simulated.
128 devices in a mesh: rows: 128 (over z, y, x, core).
Axes of the slice: x: 4, y: 4, z: 4, core: 2. Of those that a mesh axis runs over, the one named last changes fastest.
Arguments:
- events: float32 [4, 32, 1048576], P(None, None, 'rows'), may hold values from -8 to 8
- keep_indicator: int32 [4, 1048576], P(None, 'rows'), may hold values from 0 to 1, as said below
Outputs:
- lagging_mean: float32 [4, 32, 1048576], P(None, None, 'rows')
- deviation: float32 [4, 32, 1048576], P(None, None, 'rows')
Inputs may be any that keep to these rules, and one draw needn't show every extreme that they name: `keep_indicator`: in each table, each of the 128 aligned blocks of 8192 rows holds at least 4096 survivors, and some block holds exactly 4096.
All inputs are finite; a program needn't handle non-finite values.
Results may differ from a plain program's by a relative error of at most 0.0003.
Values sent between devices are 32-bit elements; how exact they have to be, the bound alone decides.
A program may use at most 128 MiB of HBM per device.

v0:
```python
import functools

import jax
import jax.numpy as jnp
from jax import lax
from jax.experimental import pallas as pl
from jax.experimental.pallas import tpu as pltpu
from jax.sharding import PartitionSpec as P

SPAN = 4096
W = 128
STREAMS = 4
COLS = 32
ROWS = 8192
TILES = ROWS // W
TABLE = ROWS + 2 * W
EARLY = SPAN + W
MESH = pl.DeviceIdType.MESH
F32 = jnp.float32
I32 = jnp.int32
BF16 = jnp.bfloat16


def lanes_of(shape):
    return lax.broadcasted_iota(I32, shape, len(shape) - 1)


def rows_of(shape):
    return lax.broadcasted_iota(I32, shape, 0)


def lane_gather(values, index):
    return jnp.take_along_axis(values, index, axis=1, mode="promise_in_bounds")


def dot(a, b):
    return jnp.dot(a, b, preferred_element_type=F32)


def make_weights(w_ref):
    r = rows_of(w_ref.shape) % W
    c = lanes_of(w_ref.shape)
    w_ref[...] = ((r <= c % W) | (c >= W)).astype(F32).astype(BF16)


def index_maps(keep_ref, keepf_ref, src_ref, rank_ref, places_ref):
    for t in range(TILES):
        keepf_ref[pl.ds(4 * t, 4), :] = keep_ref[:, t * W : (t + 1) * W].astype(F32)
    keep = keepf_ref[...].astype(BF16)
    tri = (rows_of((W, W)) <= lanes_of((W, W))).astype(F32).astype(BF16)
    ones = jnp.ones((W, W), BF16)
    inside = dot(keep, tri)
    count = dot(keep, ones).astype(BF16)
    n = TILES * STREAMS
    ri, ci = rows_of((n, n)), lanes_of((n, n))
    same = ri % STREAMS == ci % STREAMS
    before = (same & (ci // STREAMS < ri // STREAMS)).astype(F32).astype(BF16)
    after = (same & (ri // STREAMS < ci // STREAMS)).astype(F32).astype(BF16)
    same = same.astype(F32).astype(BF16)
    count_row = lax.dot_general(
        jnp.ones((8, W), BF16), keep, (((1,), (1,)), ((), ())), preferred_element_type=F32
    ).astype(BF16)
    start_row = dot(count_row, after).astype(I32)
    total_row = dot(count_row, same).astype(I32)
    sub = rows_of((8, n))
    places_ref[...] = jnp.where(
        sub == 0, start_row, jnp.where(sub == 1, start_row - total_row + ROWS, total_row)
    )
    start = dot(before, count).astype(I32)
    total = dot(same, count).astype(I32)
    inside = inside.astype(I32)
    rank_ref[...] = start + inside
    offset = (start - total) & (W - 1)
    wanted = (lanes_of((n, W)) - offset) & (W - 1)
    found = jnp.zeros((n, W), I32)
    for step in (64, 32, 16, 8, 4, 2, 1):
        probe = lane_gather(inside, found + (step - 1))
        found = jnp.where(probe <= wanted, found + step, found)
    src_ref[...] = found


def pack(s, events_ref, keepf_ref, src_ref, at, w_ref, table, prefix_ref, tail_ref, early_ref, total_ref):
    lane = lanes_of((COLS, W))
    group = 8

    def body(g, carry):
        base, current = carry
        kept, lhs = [], []
        for u in range(group):
            t = g * group + u
            x = events_ref[0, :, pl.ds(pl.multiple_of(t * W, W), W)]
            x = x * keepf_ref[pl.ds(STREAMS * t + s, 1), :]
            kept.append(x)
            hi = x.astype(BF16)
            rest = x - hi.astype(F32)
            mid = rest.astype(BF16)
            low = (rest - mid.astype(F32)).astype(BF16)
            lhs.append(jnp.concatenate([hi, mid, low], axis=1))
        sums = dot(jnp.concatenate(lhs, axis=0), w_ref[...])
        for u in range(group):
            t = g * group + u
            part = sums[u * COLS : (u + 1) * COLS]
            prefix = base + part[:, :W]
            base = base + part[:, W:]
            prefix_ref[:, pl.ds(pl.multiple_of(t * W, W), W)] = prefix
            index = jnp.broadcast_to(src_ref[pl.ds(STREAMS * t + s, 1), :], (COLS, W))
            moved = lane_gather(prefix - kept[u], index)
            place = at[1, STREAMS * t + s]
            later = jnp.where(t == TILES - 1, ROWS, at[1, jnp.minimum(STREAMS * (t + 1), STREAMS * (TILES - 1)) + s])
            block = place // W
            current = jnp.where(lane >= place % W, moved, current)
            table[:, pl.ds(pl.multiple_of(block * W, W), W)] = current
            current = jnp.where(later // W > block, moved, current)
        return base, current

    zero = jnp.zeros((COLS, W), F32)
    total, _ = lax.fori_loop(0, TILES // group, body, (zero, zero))
    total_ref[...] = total
    for t in range(SPAN // W):
        tail_ref[:, t * W : (t + 1) * W] = table[:, SPAN + t * W : SPAN + (t + 1) * W] - total
    first = ROWS - at[2, s]
    block, shift = first // W, first % W
    turn = (lane + shift) & (W - 1)
    fresh = lane < W - shift

    def rolled(j):
        return lane_gather(table[:, pl.ds(pl.multiple_of((block + j) * W, W), W)], turn)

    def early(g, now):
        for u in range(3):
            j = g * 3 + u
            following = rolled(j + 1)
            early_ref[:, pl.ds(pl.multiple_of(j * W, W), W)] = jnp.where(fresh, now, following)
            now = following
        return now

    lax.fori_loop(0, EARLY // W // 3, early, rolled(0))


def first_kernel(
    keep_ref, events_ref,
    keepf_ref, src_ref, rank_ref, places_ref, prefix_ref, tail_ref, early_ref, total_ref,
    w_ref, table, at, sem,
):
    make_weights(w_ref)
    index_maps(keep_ref, keepf_ref, src_ref, rank_ref, places_ref)
    copy = pltpu.make_async_copy(places_ref, at, sem)
    copy.start()
    copy.wait()
    pack(0, events_ref, keepf_ref, src_ref, at, w_ref, table, prefix_ref, tail_ref, early_ref, total_ref)


def pack_kernel(
    s, at, events_ref, keepf_ref, src_ref,
    prefix_ref, tail_ref, early_ref, total_ref,
    w_ref, table,
):
    make_weights(w_ref)
    pack(s, events_ref, keepf_ref, src_ref, at, w_ref, table, prefix_ref, tail_ref, early_ref, total_ref)


def shape(*dims, dtype=F32):
    return jax.ShapeDtypeStruct(dims, dtype)


VMEM = pl.BlockSpec(memory_space=pltpu.VMEM)
SMEM = pl.BlockSpec(memory_space=pltpu.SMEM)
HBM = pl.BlockSpec(memory_space=pl.ANY)
PACKED = (shape(COLS, ROWS), shape(COLS, SPAN), shape(COLS, EARLY), shape(COLS, W))
PARAMS = pltpu.CompilerParams(vmem_limit_bytes=32 * 2**20)
COST = pl.CostEstimate(flops=2_000_000_000, bytes_accessed=4 * 2**20, transcendentals=0)


def stream_block(s):
    return pl.BlockSpec((1, COLS, ROWS), lambda i: (s, 0, 0))


def whole(*dims):
    return pl.BlockSpec(dims, lambda i: (0,) * len(dims))


def pack_first(events, keep):
    n = TILES * STREAMS
    maps = (shape(n, W), shape(n, W, dtype=I32), shape(n, W, dtype=I32), shape(8, n, dtype=I32))
    outs = maps + PACKED
    return pl.pallas_call(
        first_kernel,
        grid=(1,),
        in_specs=[whole(STREAMS, ROWS), stream_block(0)],
        out_specs=[whole(*o.shape) for o in outs],
        out_shape=outs,
        scratch_shapes=[
            pltpu.VMEM((3 * W, 2 * W), BF16),
            pltpu.VMEM((COLS, TABLE), F32),
            pltpu.SMEM((8, n), I32),
            pltpu.SemaphoreType.DMA,
        ],
        compiler_params=PARAMS,
        cost_estimate=COST,
        name="pack_first",
    )(keep, events)


def pack_stream(s, places, events, keepf, src):
    n = TILES * STREAMS
    return pl.pallas_call(
        functools.partial(pack_kernel, s),
        grid=(1,),
        in_specs=[SMEM, stream_block(s), whole(n, W), whole(n, W)],
        out_specs=[whole(*o.shape) for o in PACKED],
        out_shape=PACKED,
        scratch_shapes=[pltpu.VMEM((3 * W, 2 * W), BF16), pltpu.VMEM((COLS, TABLE), F32)],
        compiler_params=PARAMS,
        cost_estimate=COST,
        name=f"pack_{s}",
    )(places, events, keepf, src)


def scan_kernel(
    places, t0, t1, t2, t3, out_ref,
    mine, half, across, plane, send, result,
    half_sem, across_sem, plane_sem, back_sem, send_sem,
):
    me = lax.axis_index("rows")
    core, chip = me % 2, me // 2
    x, zy = chip % 4, chip // 4
    even = core == 0

    def other_x(step):
        return (zy * 4 + (x + step) % 4) * 2

    def other_plane(step):
        return (((zy + step) % 16) * 4 + x) * 2

    barrier = pltpu.get_barrier_semaphore()

    def greet(device):
        pl.semaphore_signal(barrier, inc=1, device_id=(device,), device_id_type=MESH)

    greet(me + 1 - 2 * core)

    @pl.when(even)
    def _():
        for step in range(1, 4):
            greet(other_x(step))
        for step in range(1, 16):
            greet(other_plane(step))

    lane = lanes_of((8, W))
    message = jnp.zeros((8, W), F32)
    for s, total in enumerate((t0, t1, t2, t3)):
        for g in range(4):
            message = jnp.where(lane == g * 4 + s, total[g * 8 : (g + 1) * 8, :], message)
        message = jnp.where(lane == 16 + s, places[2, s].astype(F32), message)
    mine[...] = message

    def copy(src, dst, sem, k, device):
        return pltpu.make_async_remote_copy(
            src_ref=src, dst_ref=dst, send_sem=send_sem.at[k], recv_sem=sem,
            device_id=(device,), device_id_type=MESH,
        )

    @pl.when(core == 1)
    def _():
        pl.semaphore_wait(barrier, 1)
        up = copy(mine, half, half_sem, 0, me - 1)
        up.start()
        up.wait_send()
        copy(send, result, back_sem, 0, me - 1).wait_recv()
        out_ref[...] = result[...]

    @pl.when(even)
    def _():
        pl.semaphore_wait(barrier, 19)
        copy(mine, half, half_sem, 0, me + 1).wait_recv()
        both = mine[...] + half[...]
        across[0] = both
        rows = [copy(across.at[0], across.at[k], across_sem.at[k], k, other_x(k)) for k in range(1, 4)]
        for c in rows:
            c.start()
        group = both
        before = jnp.zeros((8, W), F32)
        for k in range(1, 4):
            rows[k - 1].wait_recv()
            piece = across[k]
            group = group + piece
            before = before + jnp.where((x + 4 - k) % 4 < x, piece, 0.0)
        plane[0] = group
        far = [copy(plane.at[0], plane.at[k], plane_sem.at[k], 3 + k, other_plane(k)) for k in range(1, 16)]
        for c in far:
            c.start()
        for k in range(1, 16):
            far[k - 1].wait_recv()
            before = before + jnp.where((zy + 16 - k) % 16 < zy, plane[k], 0.0)
        out_ref[...] = before
        send[...] = before + mine[...]
        back = copy(send, result, back_sem, 0, me + 1)
        back.start()
        for c in rows + far:
            c.wait_send()
        back.wait_send()


def scan(places, totals):
    tile = pltpu.VMEM((8, W), F32)
    return pl.pallas_call(
        scan_kernel,
        in_specs=[SMEM] + [VMEM] * 4,
        out_specs=VMEM,
        out_shape=shape(8, W),
        scratch_shapes=[
            tile, tile, pltpu.VMEM((4, 8, W), F32), pltpu.VMEM((16, 8, W), F32), tile, tile,
            pltpu.SemaphoreType.DMA, pltpu.SemaphoreType.DMA((4,)), pltpu.SemaphoreType.DMA((16,)),
            pltpu.SemaphoreType.DMA, pltpu.SemaphoreType.DMA((19,)),
        ],
        compiler_params=pltpu.CompilerParams(collective_id=0, has_side_effects=True),
        cost_estimate=pl.CostEstimate(flops=8_000_000_000, bytes_accessed=2**20, transcendentals=0),
        name="scan",
    )(places, *totals)


def finish_kernel(s, chunk, at, before_ref, rank_ref, prefix_ref, tail_hbm, early_hbm, *rest):
    mean_ref, deviation_ref, table, sems = rest[-4:]

    @pl.when(pl.program_id(0) == 0)
    def _():
        a = pltpu.make_async_copy(tail_hbm, table.at[:, pl.ds(0, SPAN)], sems.at[0])
        b = pltpu.make_async_copy(early_hbm, table.at[:, pl.ds(SPAN, EARLY)], sems.at[1])
        a.start()
        b.start()
        a.wait()
        b.wait()

    before = jnp.concatenate([before_ref[:, g * 4 + s : g * 4 + s + 1] for g in range(4)], axis=0)
    before = jnp.broadcast_to(before, (COLS, W))
    seen = jnp.broadcast_to(before_ref[0:1, 16 + s : 17 + s], (1, W))
    group = 4

    def body(g, _):
        for u in range(group):
            k = g * group + u
            t = pl.program_id(0) * (chunk // W) + k
            row = STREAMS * t + s
            lanes = pl.ds(pl.multiple_of(k * W, W), W)
            rank = rank_ref[pl.ds(row, 1), :]
            block = at[0, row] // W
            where = rank - block * W
            index = jnp.broadcast_to(where & (W - 1), (COLS, W))
            near = table[:, pl.ds(pl.multiple_of(block * W, W), W)]
            next_ = table[:, pl.ds(pl.multiple_of(block * W + W, W), W)]
            earlier = jnp.where(where >= W, lane_gather(next_, index), lane_gather(near, index))
            prefix = prefix_ref[:, lanes]
            mean = (prefix - earlier) * (1.0 / SPAN)
            inverse = 1.0 / jnp.maximum(seen + rank.astype(F32), 1.0)
            mean_ref[0, :, lanes] = mean
            deviation_ref[0, :, lanes] = mean - (before + prefix) * inverse
        return 0

    lax.fori_loop(0, chunk // W // group, body, 0)


def finish(s, places, before, rank, prefix, tail, early, partial_outs):
    chunk = 2048
    n = TILES * STREAMS
    block = pl.BlockSpec((1, COLS, chunk), lambda i: (s, 0, i))
    whole_out = shape(STREAMS, COLS, ROWS)
    return pl.pallas_call(
        functools.partial(finish_kernel, s, chunk),
        grid=(ROWS // chunk,),
        in_specs=[
            SMEM, whole(8, W), whole(n, W), pl.BlockSpec((COLS, chunk), lambda i: (0, i)), HBM, HBM,
        ] + [HBM] * len(partial_outs),
        out_specs=[block, block],
        out_shape=[whole_out, whole_out],
        scratch_shapes=[pltpu.VMEM((COLS, TABLE + W), F32), pltpu.SemaphoreType.DMA((2,))],
        input_output_aliases={6: 0, 7: 1} if partial_outs else {},
        compiler_params=PARAMS,
        cost_estimate=COST,
        name=f"finish_{s}",
    )(places, before, rank, prefix, tail, early, *partial_outs)


def per_device(events, keep):
    count = lax.axis_size("rows")
    chain = [(d, d + 1) for d in range(count - 1)]
    keepf, src, rank, places, *first = pack_first(events, keep)
    packed = [first]
    tails = [lax.ppermute(first[1], "rows", chain)]
    for s in range(1, STREAMS):
        packed.append(pack_stream(s, places, events, keepf, src))
        tails.append(lax.ppermute(packed[s][1], "rows", chain))
    before = scan(places, [p[3] for p in packed])
    outs = ()
    for s in range(STREAMS):
        prefix, _, early, _ = packed[s]
        outs = finish(s, places, before, rank, prefix, tails[s], early, outs)
    return tuple(outs)


def solution(mesh):
    in_specs = (P(None, None, "rows"), P(None, "rows"))
    out_specs = (P(None, None, "rows"), P(None, None, "rows"))
    return jax.shard_map(per_device, mesh=mesh, in_specs=in_specs, out_specs=out_specs, check_vma=False)
```

profile of v0, /device:TPU:1, one launch (start us, length us, event | category | flops | bytes accessed | tf_op | source)
XLA Modules:
  0.0 83.5 jit_solution(5909037060899786539)
XLA Ops:
  0.6 2.2 %copy-done.9 = f32[4,32,8192]{2,1,0:T(8,128)S(1)} copy-done((f32[4,32,8192]{2,1,0:T(8,128)S(1)}, f32[4,32,8192]{2,1,0:T(8,128)}, u32[]{:S(2)}) %copy-start.9) | copy-done | bytes 4194328
  2.8 0.9 %copy-done.11 = s32[4,8192]{1,0:T(4,128)S(1)} copy-done((s32[4,8192]{1,0:T(4,128)S(1)}, s32[4,8192]{1,0:T(4,128)}, u32[]{:S(2)}) %copy-start.11) | copy-done | bytes 131096
  3.7 5.0 %pack_first.1 = (f32[256,128]{1,0:T(8,128)S(1)}, s32[256,128]{1,0:T(8,128)S(1)}, s32[256,128]{1,0:T(8,128)S(1)}, s32[8,256]{1,0:T(8,128)S(1)}, f32[32,8192]{1,0:...) custom-call(s32[4,8192]{1,0:T(4,128)S(1)} %copy-done.11, f32[4,32,8192]{2,1,0:T(8,128)S(1)} %copy-done.9), custom_call_target="tpu_custom_call" | custom-call | flops 2000000000 | bytes 4194304 | tf_op jit(solution)/shard_map/pack_first/pallas_call | solution.py:186
  8.8 1.0 %copy-done.12 = f32[32,8192]{1,0:T(8,128)} copy-done((f32[32,8192]{1,0:T(8,128)}, f32[32,8192]{1,0:T(8,128)S(1)}, u32[]{:S(2)}) %copy-start.12) | copy-done | bytes 1048600
  9.8 0.8 copy-done.14
  10.6 4.5 %collective-permute-start.3 = (f32[32,4096]{1,0:T(8,128)}, f32[32,4096]{1,0:T(8,128)}, u32[]{:S(2)}, u32[]{:S(2)}) collective-permute-start(f32[32,4096]{1,0:T(8,128)} %get-tuple-element.46), channel_id=1, source_target_pairs={{0,1},{1,2},{2,3},{3,4},{4,5},{5,6},{6,7},{7,8},{8,9},{9,10},{10,1... | collective-permute-start | bytes 1572872 | tf_op jit(solution)/shard_map/ppermute | solution.py:388
  15.1 4.8 %pack_3.1 = (f32[32,8192]{1,0:T(8,128)S(1)}, f32[32,4096]{1,0:T(8,128)}, f32[32,4224]{1,0:T(8,128)S(1)}, f32[32,128]{1,0:T(8,128)S(1)}) custom-call(s32[8,256]{1,0:T(8,128)S(1)} %get-tuple-element.28.at.places, f32[4,32,8192]{2,1,0:T(8,128)S(1)} %copy-done.10, f32[256,128]{1,0:T(8,128)S(1)} %get-tuple-element.30.keepf_ref, ...), custom_call_target="tpu_custom_call" | custom-call | flops 2000000000 | bytes 4194304 | tf_op jit(solution)/shard_map/pack_3/pallas_call | solution.py:206
  19.8 0.8 copy-done
  21.3 1.9 %collective-permute-start = (f32[32,4096]{1,0:T(8,128)}, f32[32,4096]{1,0:T(8,128)}, u32[]{:S(2)}, u32[]{:S(2)}) collective-permute-start(f32[32,4096]{1,0:T(8,128)} %get-tuple-element.37), channel_id=1, source_target_pairs={{0,1},{1,2},{2,3},{3,4},{4,5},{5,6},{6,7},{7,8},{8,9},{9,10},{10,1... | collective-permute-start | bytes 1572872 | tf_op jit(solution)/shard_map/ppermute | solution.py:391
  23.2 4.8 %pack_2.1 = (f32[32,8192]{1,0:T(8,128)S(1)}, f32[32,4096]{1,0:T(8,128)}, f32[32,4224]{1,0:T(8,128)S(1)}, f32[32,128]{1,0:T(8,128)S(1)}) custom-call(s32[8,256]{1,0:T(8,128)S(1)} %get-tuple-element.28.at.places, f32[4,32,8192]{2,1,0:T(8,128)S(1)} %copy-done.10, f32[256,128]{1,0:T(8,128)S(1)} %get-tuple-element.30.keepf_ref, ...), custom_call_target="tpu_custom_call" | custom-call | flops 2000000000 | bytes 4194304 | tf_op jit(solution)/shard_map/pack_2/pallas_call | solution.py:206
  28.0 0.8 copy-done.2
  29.4 3.5 %collective-permute-start.1 = (f32[32,4096]{1,0:T(8,128)}, f32[32,4096]{1,0:T(8,128)}, u32[]{:S(2)}, u32[]{:S(2)}) collective-permute-start(f32[32,4096]{1,0:T(8,128)} %get-tuple-element.40), channel_id=1, source_target_pairs={{0,1},{1,2},{2,3},{3,4},{4,5},{5,6},{6,7},{7,8},{8,9},{9,10},{10,1... | collective-permute-start | bytes 1572872 | tf_op jit(solution)/shard_map/ppermute | solution.py:391
  32.9 4.8 %pack_1.1 = (f32[32,8192]{1,0:T(8,128)S(1)}, f32[32,4096]{1,0:T(8,128)}, f32[32,4224]{1,0:T(8,128)S(1)}, f32[32,128]{1,0:T(8,128)S(1)}) custom-call(s32[8,256]{1,0:T(8,128)S(1)} %get-tuple-element.28.at.places, f32[4,32,8192]{2,1,0:T(8,128)S(1)} %copy-done.10, f32[256,128]{1,0:T(8,128)S(1)} %get-tuple-element.30.keepf_ref, ...), custom_call_target="tpu_custom_call" | custom-call | flops 2000000000 | bytes 4194304 | tf_op jit(solution)/shard_map/pack_1/pallas_call | solution.py:206
  37.7 0.8 copy-done.4
  38.5 0.6 copy-done.18
  39.1 1.9 %collective-permute-start.2 = (f32[32,4096]{1,0:T(8,128)}, f32[32,4096]{1,0:T(8,128)}, u32[]{:S(2)}, u32[]{:S(2)}) collective-permute-start(f32[32,4096]{1,0:T(8,128)} %get-tuple-element.43), channel_id=1, source_target_pairs={{0,1},{1,2},{2,3},{3,4},{4,5},{5,6},{6,7},{7,8},{8,9},{9,10},{10,1... | collective-permute-start | bytes 1572872 | tf_op jit(solution)/shard_map/ppermute | solution.py:391
  41.0 18.0 %scan.1.before_ref = f32[8,128]{1,0:T(8,128)} custom-call(s32[8,256]{1,0:T(8,128)} %copy-done.6, f32[32,128]{1,0:T(8,128)} %copy-done.19, f32[32,128]{1,0:T(8,128)} %copy-done.18, f32[32,128]{1,0:T(8,128)} %copy-done.17, f32[32,128]{1,0:T(8,128)} %copy-done.16), custom_call_target="tpu_custom_call" | custom-call | flops 8000000000 | bytes 1048576 | tf_op jit(solution)/shard_map/scan/pallas_call | solution.py:306
  59.0 0.7 copy-done.8
  59.7 1.2 %copy-done.13 = f32[32,8192]{1,0:T(8,128)S(1)} copy-done((f32[32,8192]{1,0:T(8,128)S(1)}, f32[32,8192]{1,0:T(8,128)}, u32[]{:S(2)}) %copy-start.13) | copy-done | bytes 1048600
  61.0 1.0 %copy-done.15 = f32[32,4224]{1,0:T(8,128)S(1)} copy-done((f32[32,4224]{1,0:T(8,128)S(1)}, f32[32,4224]{1,0:T(8,128)}, u32[]{:S(2)}) %copy-start.15) | copy-done | bytes 540696
  62.0 5.3 %finish_0.1 = (f32[4,32,8192]{2,1,0:T(8,128)}, f32[4,32,8192]{2,1,0:T(8,128)}) custom-call(s32[8,256]{1,0:T(8,128)S(1)} %copy-done.7, f32[8,128]{1,0:T(8,128)S(1)} %copy-done.8, s32[256,128]{1,0:T(8,128)S(1)} %get-tuple-element.35.rank_ref, f32[32,8192]{1,0:T(8,128)S(1)} %copy-done.13, f32[32,4096]{1,0:T(8,128)} %collective-permute-done.3.tail_hbm, ...), custom_call_target="tpu_custom_call" | custom-call | flops 2000000000 | bytes 4194304 | tf_op jit(solution)/shard_map/finish_0/pallas_call | solution.py:367
  67.4 5.4 %finish_1.1 = (f32[4,32,8192]{2,1,0:T(8,128)}, f32[4,32,8192]{2,1,0:T(8,128)}) custom-call(s32[8,256]{1,0:T(8,128)S(1)} %copy-done.7, f32[8,128]{1,0:T(8,128)S(1)} %copy-done.8, s32[256,128]{1,0:T(8,128)S(1)} %get-tuple-element.35.rank_ref, f32[32,8192]{1,0:T(8,128)S(1)} %get-tuple-element.42.prefix_ref, ...), custom_call_target="tpu_custom_call", output_to_operand_aliasing={{0}: (6, {}), {1}: (7, {})} | custom-call | flops 2000000000 | bytes 4194304 | tf_op jit(solution)/shard_map/finish_1/pallas_call | solution.py:367
  72.8 5.4 %finish_2.1 = (f32[4,32,8192]{2,1,0:T(8,128)}, f32[4,32,8192]{2,1,0:T(8,128)}) custom-call(s32[8,256]{1,0:T(8,128)S(1)} %copy-done.7, f32[8,128]{1,0:T(8,128)S(1)} %copy-done.8, s32[256,128]{1,0:T(8,128)S(1)} %get-tuple-element.35.rank_ref, f32[32,8192]{1,0:T(8,128)S(1)} %get-tuple-element.39.prefix_ref, ...), custom_call_target="tpu_custom_call", output_to_operand_aliasing={{0}: (6, {}), {1}: (7, {})} | custom-call | flops 2000000000 | bytes 4194304 | tf_op jit(solution)/shard_map/finish_2/pallas_call | solution.py:367
  78.2 5.4 %finish_3.1 = (f32[4,32,8192]{2,1,0:T(8,128)}, f32[4,32,8192]{2,1,0:T(8,128)}) custom-call(s32[8,256]{1,0:T(8,128)S(1)} %copy-done.7, f32[8,128]{1,0:T(8,128)S(1)} %copy-done.8, s32[256,128]{1,0:T(8,128)S(1)} %get-tuple-element.35.rank_ref, f32[32,8192]{1,0:T(8,128)S(1)} %get-tuple-element.36.prefix_ref, ...), custom_call_target="tpu_custom_call", output_to_operand_aliasing={{0}: (6, {}), {1}: (7, {})} | custom-call | flops 2000000000 | bytes 4194304 | tf_op jit(solution)/shard_map/finish_3/pallas_call | solution.py:367
  (33 shorter events, 1.3 us)
Async XLA Ops:
  0.6 2.2 %copy-start.9 = (f32[4,32,8192]{2,1,0:T(8,128)S(1)}, f32[4,32,8192]{2,1,0:T(8,128)}, u32[]{:S(2)}) copy-start(f32[4,32,8192]{2,1,0:T(8,128)} %events_ref.7) | copy-start | bytes 12582916
  2.8 0.9 %copy-start.11 = (s32[4,8192]{1,0:T(4,128)S(1)}, s32[4,8192]{1,0:T(4,128)}, u32[]{:S(2)}) copy-start(s32[4,8192]{1,0:T(4,128)} %keep_ref.1) | copy-start | bytes 393220
  3.7 11.3 %copy-start.10 = (f32[4,32,8192]{2,1,0:T(8,128)S(1)}, f32[4,32,8192]{2,1,0:T(8,128)}, u32[]{:S(2)}) copy-start(f32[4,32,8192]{2,1,0:T(8,128)} %events_ref.7) | copy-start | bytes 12582916
  8.8 1.0 %copy-start.12 = (f32[32,8192]{1,0:T(8,128)}, f32[32,8192]{1,0:T(8,128)S(1)}, u32[]{:S(2)}) copy-start(f32[32,8192]{1,0:T(8,128)S(1)} %get-tuple-element.45.prefix_ref) | copy-start | bytes 3145732
  9.7 0.8 copy-start.14
  10.5 17.4 %copy-start.19 = (f32[32,128]{1,0:T(8,128)}, f32[32,128]{1,0:T(8,128)S(1)}, u32[]{:S(2)}) copy-start(f32[32,128]{1,0:T(8,128)S(1)} %get-tuple-element.29.t0) | copy-start | bytes 49156
  10.5 22.3 %copy-start.6 = (s32[8,256]{1,0:T(8,128)}, s32[8,256]{1,0:T(8,128)S(1)}, u32[]{:S(2)}) copy-start(s32[8,256]{1,0:T(8,128)S(1)} %get-tuple-element.28.at.places) | copy-start | bytes 24580
  10.6 48.4 %collective-permute-start.3 = (f32[32,4096]{1,0:T(8,128)}, f32[32,4096]{1,0:T(8,128)}, u32[]{:S(2)}, u32[]{:S(2)}) collective-permute-start(f32[32,4096]{1,0:T(8,128)} %get-tuple-element.46), channel_id=1, source_target_pairs={{0,1},{1,2},{2,3},{3,4},{4,5},{5,6},{6,7},{7,8},{8,9},{9,10},{10,1... | collective-permute-start | bytes 1572872 | tf_op jit(solution)/shard_map/ppermute | solution.py:388
  19.8 0.8 copy-start
  20.7 0.6 copy-start.16
  21.3 56.9 %collective-permute-start = (f32[32,4096]{1,0:T(8,128)}, f32[32,4096]{1,0:T(8,128)}, u32[]{:S(2)}, u32[]{:S(2)}) collective-permute-start(f32[32,4096]{1,0:T(8,128)} %get-tuple-element.37), channel_id=1, source_target_pairs={{0,1},{1,2},{2,3},{3,4},{4,5},{5,6},{6,7},{7,8},{8,9},{9,10},{10,1... | collective-permute-start | bytes 1572872 | tf_op jit(solution)/shard_map/ppermute | solution.py:391
  28.0 0.8 copy-start.2
  28.8 0.6 copy-start.17
  29.4 43.4 %collective-permute-start.1 = (f32[32,4096]{1,0:T(8,128)}, f32[32,4096]{1,0:T(8,128)}, u32[]{:S(2)}, u32[]{:S(2)}) collective-permute-start(f32[32,4096]{1,0:T(8,128)} %get-tuple-element.40), channel_id=1, source_target_pairs={{0,1},{1,2},{2,3},{3,4},{4,5},{5,6},{6,7},{7,8},{8,9},{9,10},{10,1... | collective-permute-start | bytes 1572872 | tf_op jit(solution)/shard_map/ppermute | solution.py:391
  37.7 0.8 copy-start.4
  38.5 0.6 copy-start.18
  39.1 28.3 %collective-permute-start.2 = (f32[32,4096]{1,0:T(8,128)}, f32[32,4096]{1,0:T(8,128)}, u32[]{:S(2)}, u32[]{:S(2)}) collective-permute-start(f32[32,4096]{1,0:T(8,128)} %get-tuple-element.43), channel_id=1, source_target_pairs={{0,1},{1,2},{2,3},{3,4},{4,5},{5,6},{6,7},{7,8},{8,9},{9,10},{10,1... | collective-permute-start | bytes 1572872 | tf_op jit(solution)/shard_map/ppermute | solution.py:391
  41.0 18.0 %copy-start.7 = (s32[8,256]{1,0:T(8,128)S(1)}, s32[8,256]{1,0:T(8,128)}, u32[]{:S(2)}) copy-start(s32[8,256]{1,0:T(8,128)} %copy-done.6) | copy-start | bytes 24580
  59.0 8.4 %copy-start.5 = (f32[32,4224]{1,0:T(8,128)S(1)}, f32[32,4224]{1,0:T(8,128)}, u32[]{:S(2)}) copy-start(f32[32,4224]{1,0:T(8,128)} %copy-done.4) | copy-start | bytes 1622020
  59.0 0.7 copy-start.8
  59.7 1.2 %copy-start.13 = (f32[32,8192]{1,0:T(8,128)S(1)}, f32[32,8192]{1,0:T(8,128)}, u32[]{:S(2)}) copy-start(f32[32,8192]{1,0:T(8,128)} %copy-done.12) | copy-start | bytes 3145732
  61.0 1.0 %copy-start.15 = (f32[32,4224]{1,0:T(8,128)S(1)}, f32[32,4224]{1,0:T(8,128)}, u32[]{:S(2)}) copy-start(f32[32,4224]{1,0:T(8,128)} %copy-done.14) | copy-start | bytes 1622020
  67.4 5.4 %copy-start.3 = (f32[32,4224]{1,0:T(8,128)S(1)}, f32[32,4224]{1,0:T(8,128)}, u32[]{:S(2)}) copy-start(f32[32,4224]{1,0:T(8,128)} %copy-done.2) | copy-start | bytes 1622020
  72.8 5.4 %copy-start.1 = (f32[32,4224]{1,0:T(8,128)S(1)}, f32[32,4224]{1,0:T(8,128)}, u32[]{:S(2)}) copy-start(f32[32,4224]{1,0:T(8,128)} %copy-done) | copy-start | bytes 1622020
where the time goes:
time: 84.1 us; the launch traced here: 83.5 us
  Pallas kernels  58.8 us (70%)
  local copies, waits for them, and re-layouts  12.1 us (14%)
  starting transfers between devices  11.8 us (14%)
  between operations  0.85 us (1%)
    pallas_call x4, Pallas kernels, finish(): pl.pallas_call(functools.partial(finish_kernel, s, chunk), grid=(ROWS //...  21.4 us
    pallas_call x1, Pallas kernels, scan(): pl.pallas_call(scan_kernel, in_specs=[SMEM] + [VMEM] * 4, out_specs=VMEM,...  18 us
    pallas_call x3, Pallas kernels, pack_stream(): pl.pallas_call(functools.partial(pack_kernel, s), grid=(1,), in_specs=[SM...  14.4 us
    unnamed x40, local copies, waits for them, and re-layouts  12.1 us
    ppermute x3, starting transfers between devices, per_device(): tails.append(lax.ppermute(packed[s][1], 'rows', chain))  7.31 us
    pallas_call x1, Pallas kernels, pack_first(): pl.pallas_call(first_kernel, grid=(1,), in_specs=[whole(STREAMS, ROWS), s...  5.04 us
    ppermute x1, starting transfers between devices, per_device(): tails = [lax.ppermute(first[1], 'rows', chain)]  4.49 us
  transfers between devices with their start and end apart: 4, of which 0 were waited for; matrix products, arithmetic and copies ran while one was open for 0% of the time, Pallas kernels for 58%

commit v1 on v0

v1 whole, which is shorter than its diff:
```python
import jax
import jax.numpy as jnp
from jax import lax
from jax.experimental import pallas as pl
from jax.experimental.pallas import tpu as pltpu
from jax.sharding import PartitionSpec as P

SPAN = 4096
W = 128
STREAMS = 4
COLS = 32
ROWS = 8192
TILES = ROWS // W
LEAD = 8
TABLE = TILES + LEAD + 2
EARLY = SPAN + W
N = TILES * STREAMS
MESH = pl.DeviceIdType.MESH
F32 = jnp.float32
I32 = jnp.int32
BF16 = jnp.bfloat16


def lanes_of(shape):
    return lax.broadcasted_iota(I32, shape, len(shape) - 1)


def rows_of(shape):
    return lax.broadcasted_iota(I32, shape, 0)


def lane_gather(values, index):
    return jnp.take_along_axis(values, index, axis=1, mode="promise_in_bounds")


def dot(a, b):
    return jnp.dot(a, b, preferred_element_type=F32)


def make_weights(w_ref):
    r = rows_of(w_ref.shape) % W
    c = lanes_of(w_ref.shape)
    w_ref[...] = ((r <= c % W) | (c >= W)).astype(F32).astype(BF16)


def index_maps(keep_ref, keepi_ref, keepf_ref, src_ref, rank_ref, places_ref, moves_ref):
    for t in range(TILES):
        keepi_ref[pl.ds(STREAMS * t, STREAMS), :] = keep_ref[:, t * W : (t + 1) * W]
    keep = keepi_ref[...].astype(F32)
    keepf_ref[...] = keep
    keep = keep.astype(BF16)
    tri = (rows_of((W, W)) <= lanes_of((W, W))).astype(F32).astype(BF16)
    ones = jnp.ones((W, W), BF16)
    inside = dot(keep, tri)
    count = dot(keep, ones)
    counts = count.astype(BF16)
    ri, ci = rows_of((N, N)), lanes_of((N, N))
    same = (ri & (STREAMS - 1)) == (ci & (STREAMS - 1))
    before = (same & ((ci >> 2) < (ri >> 2))).astype(F32).astype(BF16)
    same = same.astype(F32).astype(BF16)
    count_row = jnp.sum(keepi_ref[...].T, axis=0, keepdims=True)
    count_row = jnp.broadcast_to(count_row, (8, N))
    start_row = count_row
    for k in range(6):
        step = STREAMS << k
        start_row = start_row + jnp.where(lanes_of((8, N)) >= step, pltpu.roll(start_row, step, 1), 0)
    places_ref[...] = jnp.where(rows_of((8, N)) == 0, start_row - count_row, start_row)
    start = dot(before, counts).astype(I32)
    total = dot(same, counts).astype(I32)
    inside = inside.astype(I32)
    rank_ref[...] = start + inside
    place = start - total + ROWS
    wanted = (lanes_of((N, W)) - place) & (W - 1)
    way = jnp.where(wanted < count.astype(I32), ((place + wanted) >> 7) - (rows_of((N, W)) >> 2), 0)
    for k in range(6):
        step = STREAMS << k
        moves = (way >> k) & 1
        moves_ref[k, STREAMS * LEAD :, :] = moves
        moves_ref[k, : STREAMS * LEAD, :] = jnp.zeros((STREAMS * LEAD, W), I32)
        arrives = pltpu.roll(moves, step, 0)
        way = jnp.where(arrives == 1, pltpu.roll(way, step, 0), jnp.where(moves == 1, 0, way))
    found = jnp.zeros((N, W), I32)
    for step in (64, 32, 16, 8, 4, 2, 1):
        probe = lane_gather(inside, found + (step - 1))
        found = jnp.where(probe <= wanted, found + step, found)
    src_ref[...] = found
    return total[0:8, :].astype(F32)


def prefixes(s, events_ref, keepf_ref, w_ref, prefix_ref, exclusive):
    group = 16

    def body(g, base):
        kept, lhs = [], []
        for u in range(group):
            t = g * group + u
            x = events_ref[:, pl.ds(pl.multiple_of(t * W, W), W)]
            x = x * keepf_ref[pl.ds(STREAMS * t + s, 1), :]
            kept.append(x)
            hi = x.astype(BF16)
            lhs.append(jnp.concatenate([hi, (x - hi.astype(F32)).astype(BF16)], axis=1))
        sums = dot(jnp.concatenate(lhs, axis=0), w_ref[...])
        for u in range(group):
            part = sums[u * COLS : (u + 1) * COLS]
            prefix = base + part[:, :W]
            base = base + part[:, W:]
            prefix_ref[g * group + u] = prefix
            exclusive[g * group + u] = prefix - kept[u]
        return base

    return lax.fori_loop(0, TILES // group, body, jnp.zeros((COLS, W), F32))


def tile_at(t):
    return pl.ds(pl.multiple_of(t * W, W), W)


def compact(s, src_ref, moves_ref, exclusive, table):
    group = 16

    def gather(g, _):
        for u in range(group):
            t = g * group + u
            index = jnp.broadcast_to(src_ref[pl.ds(STREAMS * t + s, 1), :], (COLS, W))
            table[t + LEAD] = lane_gather(exclusive[t], index)
        return 0

    lax.fori_loop(0, TILES // group, gather, 0)
    for k in range(6):
        step = 1 << k
        blocks = (TILES - step) // LEAD if step >= LEAD else TILES // LEAD

        def shift(g, _):
            moved = []
            for u in range(LEAD):
                t = TILES - 1 - g * LEAD - u
                moves = moves_ref[k, pl.ds(STREAMS * (t - step + LEAD) + s, 1), :]
                moved.append(
                    jnp.where(moves == 1, table[t - step + LEAD], table[t + LEAD])
                )
            for u in range(LEAD):
                table[TILES - 1 - g * LEAD - u + LEAD] = moved[u]
            return 0

        lax.fori_loop(0, blocks, shift, 0)


def take_tail(table, total, tail_ref):
    for t in range(SPAN // W):
        tail_ref[t] = table[LEAD + SPAN // W + t] - total


def take_early(s, at, table, windows):
    lane = lanes_of((COLS, W))
    first = ROWS - at[1, N - STREAMS + s]
    block, shift = jnp.minimum(first >> 7, SPAN // W), first & (W - 1)
    turn = (lane + shift) & (W - 1)
    fresh = lane < W - shift

    def rolled(j):
        return lane_gather(table[block + j + LEAD], turn)

    def early(g, now):
        for u in range(11):
            j = g * 11 + u
            following = rolled(j + 1)
            windows[SPAN // W + j] = jnp.where(fresh, now, following)
            now = following
        return now

    lax.fori_loop(0, EARLY // W // 11, early, rolled(0))


def finish(s, at, notes, rank_ref, prefix_ref, windows, mean_ref, deviation_ref):
    before = jnp.concatenate([notes[:, g * 4 + s : g * 4 + s + 1] for g in range(4)], axis=0)
    before = jnp.broadcast_to(before, (COLS, W))
    seen = jnp.broadcast_to(notes[0:1, 16 + s : 17 + s], (1, W))
    group = 16

    def body(g, _):
        for u in range(group):
            t = g * group + u
            row = STREAMS * t + s
            rank = rank_ref[pl.ds(row, 1), :]
            block = at[0, row] >> 7
            where = rank - (block << 7)
            index = jnp.broadcast_to(where & (W - 1), (COLS, W))
            near = windows[block]
            next_ = windows[block + 1]
            earlier = jnp.where(where >= W, lane_gather(next_, index), lane_gather(near, index))
            prefix = prefix_ref[t]
            mean = (prefix - earlier) * (1.0 / SPAN)
            inverse = 1.0 / jnp.maximum(seen + rank.astype(F32), 1.0)
            mean_ref[:, tile_at(t)] = mean
            deviation_ref[:, tile_at(t)] = mean - (before + prefix) * inverse
        return 0

    lax.fori_loop(0, TILES // group, body, 0)


def kernel(
    keep_hbm, events_hbm,
    mean_ref, deviation_ref,
    keep_ref, events, w_ref, keepi_ref, keepf_ref, src_ref, rank_ref, places_ref, moves_ref, at,
    prefix_ref, exclusive, table, tail, windows0, windows1, windows2, windows3,
    mine, half, across, plane, send, result,
    local_sem, tail_send, tail_recv, half_sem, across_sem, plane_sem, back_sem, scan_send,
):
    windows = (windows0, windows1, windows2, windows3)
    loads = [pltpu.make_async_copy(keep_hbm, keep_ref, local_sem.at[0])]
    for s in range(STREAMS):
        loads.append(pltpu.make_async_copy(events_hbm.at[s], events.at[s], local_sem.at[1 + s]))
    for load in loads:
        load.start()
    devices = lax.axis_size("rows")
    me = lax.axis_index("rows")
    core, chip = me % 2, me // 2
    x, zy = chip % 4, chip // 4
    even = core == 0

    def other_x(step):
        return (zy * 4 + (x + step) % 4) * 2

    def other_plane(step):
        return (((zy + step) % 16) * 4 + x) * 2

    barrier = pltpu.get_barrier_semaphore()

    def greet(device):
        pl.semaphore_signal(barrier, inc=1, device_id=(device,), device_id_type=MESH)

    def remote(src, dst, send_sem, recv_sem, device):
        return pltpu.make_async_remote_copy(
            src_ref=src, dst_ref=dst, send_sem=send_sem, recv_sem=recv_sem,
            device_id=(device,), device_id_type=MESH,
        )

    following = jnp.minimum(me + 1, devices - 1)

    @pl.when(me > 0)
    def _():
        greet(me - 1)

    @pl.when(me < devices - 1)
    def _():
        greet(me + 1)

    @pl.when(even)
    def _():
        for step in range(1, 4):
            greet(other_x(step))
        for step in range(1, 16):
            greet(other_plane(step))

    make_weights(w_ref)
    loads[0].wait()
    totals = index_maps(keep_ref, keepi_ref, keepf_ref, src_ref, rank_ref, places_ref, moves_ref)
    places = pltpu.make_async_copy(places_ref, at, local_sem.at[5])
    places.start()

    @pl.when(me == 0)
    def _():
        pl.semaphore_wait(barrier, 19)

    @pl.when((me > 0) & even)
    def _():
        pl.semaphore_wait(barrier, 20)

    @pl.when((core == 1) & (me < devices - 1))
    def _():
        pl.semaphore_wait(barrier, 2)

    @pl.when(me == devices - 1)
    def _():
        pl.semaphore_wait(barrier, 1)

    def tail_copy(s):
        return remote(
            tail.at[s], windows[s].at[pl.ds(0, SPAN // W)], tail_send.at[s], tail_recv.at[s], following
        )

    lane = lanes_of((8, W))
    message = jnp.zeros((8, W), F32)
    for s in range(STREAMS):
        loads[1 + s].wait()
        total = prefixes(s, events.at[s], keepf_ref, w_ref, prefix_ref.at[s], exclusive)
        compact(s, src_ref, moves_ref, exclusive, table)
        take_tail(table, total, tail.at[s])

        @pl.when(me < devices - 1)
        def _():
            tail_copy(s).start()

        if s == 0:
            places.wait()
        take_early(s, at, table, windows[s])
        for g in range(4):
            message = jnp.where(lane == g * 4 + s, total[g * 8 : (g + 1) * 8, :], message)
        message = jnp.where(lane == 16 + s, totals[s : s + 1, :], message)
    mine[...] = message

    @pl.when(core == 1)
    def _():
        up = remote(mine, half, scan_send.at[0], half_sem, me - 1)
        up.start()
        up.wait_send()
        remote(send, result, scan_send.at[0], back_sem, me - 1).wait_recv()

    @pl.when(even)
    def _():
        remote(mine, half, scan_send.at[0], half_sem, me + 1).wait_recv()
        both = mine[...] + half[...]
        across[0] = both
        rows = [
            remote(across.at[0], across.at[k], scan_send.at[k], across_sem.at[k], other_x(k))
            for k in range(1, 4)
        ]
        for c in rows:
            c.start()
        group = both
        before = jnp.zeros((8, W), F32)
        for k in range(1, 4):
            rows[k - 1].wait_recv()
            piece = across[k]
            group = group + piece
            before = before + jnp.where((x + 4 - k) % 4 < x, piece, 0.0)
        plane[0] = group
        far = [
            remote(plane.at[0], plane.at[k], scan_send.at[3 + k], plane_sem.at[k], other_plane(k))
            for k in range(1, 16)
        ]
        for c in far:
            c.start()
        for k in range(1, 16):
            far[k - 1].wait_recv()
            before = before + jnp.where((zy + 16 - k) % 16 < zy, plane[k], 0.0)
        result[...] = before
        send[...] = before + mine[...]
        back = remote(send, result, scan_send.at[0], back_sem, me + 1)
        back.start()
        for c in rows + far:
            c.wait_send()
        back.wait_send()

    notes = result[...]

    @pl.when(me == 0)
    def _():
        for s in range(STREAMS):
            for t in range(SPAN // W):
                windows[s][t] = jnp.zeros((COLS, W), F32)

    for s in range(STREAMS):

        @pl.when(me > 0)
        def _():
            tail_copy(s).wait_recv()

        finish(s, at, notes, rank_ref, prefix_ref.at[s], windows[s], mean_ref.at[s], deviation_ref.at[s])

    @pl.when(me < devices - 1)
    def _():
        for s in range(STREAMS):
            tail_copy(s).wait_send()


def per_device(events, keep):
    out = jax.ShapeDtypeStruct((STREAMS, COLS, ROWS), F32)
    tile = pltpu.VMEM((8, W), F32)
    dma = pltpu.SemaphoreType.DMA
    hbm = pl.BlockSpec(memory_space=pltpu.HBM)
    vmem = pl.BlockSpec(memory_space=pltpu.VMEM)
    return pl.pallas_call(
        kernel,
        in_specs=[hbm, hbm],
        out_specs=[vmem, vmem],
        out_shape=[out, out],
        scratch_shapes=[
            pltpu.VMEM((STREAMS, ROWS), I32),
            pltpu.VMEM((STREAMS, COLS, ROWS), F32),
            pltpu.VMEM((2 * W, 2 * W), BF16),
            pltpu.VMEM((N, W), I32),
            pltpu.VMEM((N, W), F32),
            pltpu.VMEM((N, W), I32),
            pltpu.VMEM((N, W), I32),
            pltpu.VMEM((8, N), I32),
            pltpu.VMEM((6, N + STREAMS * LEAD, W), I32),
            pltpu.SMEM((8, N), I32),
            pltpu.VMEM((STREAMS, TILES, COLS, W), F32),
            pltpu.VMEM((TILES, COLS, W), F32),
            pltpu.VMEM((TABLE, COLS, W), F32),
            pltpu.VMEM((STREAMS, SPAN // W, COLS, W), F32),
        ]
        + [pltpu.VMEM((TILES + 3, COLS, W), F32)] * STREAMS
        + [
            tile, tile, pltpu.VMEM((4, 8, W), F32), pltpu.VMEM((16, 8, W), F32), tile, tile,
            dma((6,)), dma((STREAMS,)), dma((STREAMS,)), dma, dma((4,)), dma((16,)), dma, dma((19,)),
        ],
        compiler_params=pltpu.CompilerParams(
            collective_id=0, has_side_effects=True, vmem_limit_bytes=44 * 2**20
        ),
        name="windows",
    )(keep, events)


def solution(mesh):
    in_specs = (P(None, None, "rows"), P(None, "rows"))
    out_specs = (P(None, None, "rows"), P(None, None, "rows"))
    return jax.shard_map(per_device, mesh=mesh, in_specs=in_specs, out_specs=out_specs, check_vma=False)
```

time: 84.1 us -> 49.6 us (0.59)
  Pallas kernels: 58.8 us -> 43.9 us
  starting transfers between devices: 11.8 us -> 0 us
  local copies, waits for them, and re-layouts: 12.1 us -> 4.93 us
    pallas_call x9 -> x1, Pallas kernels: 58.8 us -> 43.9 us  [per_device(): pl.pallas_call(kernel, in_specs=[hbm, hbm], out_specs=[vmem, vmem], out_s...]
    ppermute x4 -> x0, starting transfers between devices: 11.8 us -> none  [the longest x3 7.31 us: per_device(): tails.append(lax.ppermute(packed[s][1], 'rows', chain))]
    unnamed x40 -> x4, local copies, waits for them, and re-layouts: 12.1 us -> 4.93 us
  transfers between devices with their start and end apart: 4 -> 0, of which waited for: 0 -> 0; matrix products, arithmetic and copies ran while one was open for 0% -> 0% of each run, Pallas kernels for 58% -> 0%
where the time goes in v1:
time: 49.6 us; the launch traced here: 49.5 us
  Pallas kernels  43.9 us (89%)
  local copies, waits for them, and re-layouts  4.93 us (10%)
  between operations  0.65 us (1%)
    pallas_call x1, Pallas kernels, per_device(): pl.pallas_call(kernel, in_specs=[hbm, hbm], out_specs=[vmem, vmem], out_s...  43.9 us
    unnamed x4, local copies, waits for them, and re-layouts  4.93 us

profile of v1, /device:TPU:1, one launch (start us, length us, event | category | flops | bytes accessed | tf_op | source)
XLA Modules:
  0.0 49.5 jit_solution(18324456001571576537)
XLA Ops:
  0.6 0.0 copy-start
  0.6 0.9 %copy-done = s32[4,8192]{1,0:T(4,128)S(1)} copy-done((s32[4,8192]{1,0:T(4,128)S(1)}, s32[4,8192]{1,0:T(4,128)}, u32[]{:S(2)}) %copy-start) | copy-done | bytes 131096
  1.5 43.9 %windows.1 = (f32[4,32,8192]{2,1,0:T(8,128)S(1)}, f32[4,32,8192]{2,1,0:T(8,128)S(1)}) custom-call(s32[4,8192]{1,0:T(4,128)S(1)} %copy-done, f32[4,32,8192]{2,1,0:T(8,128)} %events_hbm.1), custom_call_target="tpu_custom_call" | custom-call | tf_op jit(solution)/shard_map/windows/pallas_call | solution.py:373
  45.4 2.0 %copy.6 = f32[4,32,8192]{2,1,0:T(8,128)} copy(f32[4,32,8192]{2,1,0:T(8,128)S(1)} %get-tuple-element.4) | data formatting | bytes 8388608
  47.4 2.0 %copy.7 = f32[4,32,8192]{2,1,0:T(8,128)} copy(f32[4,32,8192]{2,1,0:T(8,128)S(1)} %get-tuple-element.5) | data formatting | bytes 8388608
Async XLA Ops:
  0.6 0.9 %copy-start = (s32[4,8192]{1,0:T(4,128)S(1)}, s32[4,8192]{1,0:T(4,128)}, u32[]{:S(2)}) copy-start(s32[4,8192]{1,0:T(4,128)} %keep_hbm.1) | copy-start | bytes 393220

commit v2 on v1

--- a/solution.py
+++ b/solution.py
@@ -15,6 +15,11 @@
 TABLE = TILES + LEAD + 2
 EARLY = SPAN + W
 N = TILES * STREAMS
+UNITS = ((0, 3), (0, 2), (1, 3), (1, 2))
+BACK = [[g for t, g in UNITS if t == s] for s in range(STREAMS)]
+RELAYS_MIDDLE = ((), (), ((1, 1),), ((2, 1), (1, 2)))
+RELAYS = ((), ((0, 1),), ((0, 2),), ((3, 1), (2, 2), (3, 2)))
+ORDER = (2, 0, 1, 3)
 MESH = pl.DeviceIdType.MESH
 F32 = jnp.float32
 I32 = jnp.int32
@@ -58,13 +63,17 @@
     same = (ri & (STREAMS - 1)) == (ci & (STREAMS - 1))
     before = (same & ((ci >> 2) < (ri >> 2))).astype(F32).astype(BF16)
     same = same.astype(F32).astype(BF16)
-    count_row = jnp.sum(keepi_ref[...].T, axis=0, keepdims=True)
+    turned = keepi_ref[...].T
+    count_row = jnp.sum(turned, axis=0, keepdims=True)
     count_row = jnp.broadcast_to(count_row, (8, N))
     start_row = count_row
     for k in range(6):
         step = STREAMS << k
         start_row = start_row + jnp.where(lanes_of((8, N)) >= step, pltpu.roll(start_row, step, 1), 0)
-    places_ref[...] = jnp.where(rows_of((8, N)) == 0, start_row - count_row, start_row)
+    start_row = start_row - count_row
+    sub = rows_of((8, N))
+    first_row = jnp.broadcast_to(turned[0:1], (8, N))
+    places_ref[...] = start_row + jnp.where(sub == 1, count_row, jnp.where(sub == 2, first_row, 0))
     start = dot(before, counts).astype(I32)
     total = dot(same, counts).astype(I32)
     inside = inside.astype(I32)
@@ -175,6 +184,7 @@
     before = jnp.concatenate([notes[:, g * 4 + s : g * 4 + s + 1] for g in range(4)], axis=0)
     before = jnp.broadcast_to(before, (COLS, W))
     seen = jnp.broadcast_to(notes[0:1, 16 + s : 17 + s], (1, W))
+    lane = lanes_of((COLS, W))
     group = 16
 
     def body(g, _):
@@ -183,11 +193,9 @@
             row = STREAMS * t + s
             rank = rank_ref[pl.ds(row, 1), :]
             block = at[0, row] >> 7
-            where = rank - (block << 7)
-            index = jnp.broadcast_to(where & (W - 1), (COLS, W))
-            near = windows[block]
-            next_ = windows[block + 1]
-            earlier = jnp.where(where >= W, lane_gather(next_, index), lane_gather(near, index))
+            index = jnp.broadcast_to(rank & (W - 1), (COLS, W))
+            slots = jnp.where(lane >= at[2, row] - (block << 7), windows[block], windows[block + 1])
+            earlier = lane_gather(slots, index)
             prefix = prefix_ref[t]
             mean = (prefix - earlier) * (1.0 / SPAN)
             inverse = 1.0 / jnp.maximum(seen + rank.astype(F32), 1.0)
@@ -198,19 +206,43 @@
     lax.fori_loop(0, TILES // group, body, 0)
 
 
+def take_message(events, keepf_ref, totals):
+    group = 4
+
+    def body(g, sums):
+        sums = list(sums)
+        for u in range(group):
+            t = g * group + u
+            for s in range(STREAMS):
+                sums[s] = sums[s] + events[s, :, tile_at(t)] * keepf_ref[pl.ds(STREAMS * t + s, 1), :]
+        return tuple(sums)
+
+    zero = jnp.zeros((COLS, W), F32)
+    sums = lax.fori_loop(0, TILES // group, body, (zero,) * STREAMS)
+    lane = lanes_of((8, W))
+    message = jnp.zeros((8, W), F32)
+    for s in range(STREAMS):
+        total = jnp.sum(sums[s], axis=1, keepdims=True)
+        for g in range(4):
+            message = jnp.where(lane == g * 4 + s, total[g * 8 : (g + 1) * 8], message)
+        message = jnp.where(lane == 16 + s, totals[s : s + 1, :], message)
+    return message
+
+
 def kernel(
-    keep_hbm, events_hbm,
+    keep_ref, events_hbm,
     mean_ref, deviation_ref,
-    keep_ref, events, w_ref, keepi_ref, keepf_ref, src_ref, rank_ref, places_ref, moves_ref, at,
+    events, w_ref, keepi_ref, keepf_ref, src_ref, rank_ref, places_ref, moves_ref, at,
     prefix_ref, exclusive, table, tail, windows0, windows1, windows2, windows3,
-    mine, half, across, plane, send, result,
-    local_sem, tail_send, tail_recv, half_sem, across_sem, plane_sem, back_sem, scan_send,
+    relay, mine, half, across, plane, inside, given, send, result,
+    local_sem, tail_send, tail_recv, half_sem, across_sem, plane_sem, given_sem, back_sem, scan_send,
+    hop_send, hop_recv,
 ):
     windows = (windows0, windows1, windows2, windows3)
-    loads = [pltpu.make_async_copy(keep_hbm, keep_ref, local_sem.at[0])]
+    loads = [None]
     for s in range(STREAMS):
         loads.append(pltpu.make_async_copy(events_hbm.at[s], events.at[s], local_sem.at[1 + s]))
-    for load in loads:
+    for load in loads[1:]:
         load.start()
     devices = lax.axis_size("rows")
     me = lax.axis_index("rows")
@@ -235,112 +267,195 @@
             device_id=(device,), device_id_type=MESH,
         )
 
-    following = jnp.minimum(me + 1, devices - 1)
-
-    @pl.when(me > 0)
-    def _():
-        greet(me - 1)
-
-    @pl.when(me < devices - 1)
-    def _():
-        greet(me + 1)
+    following, preceding = (me + 1) % devices, (me + devices - 1) % devices
+    ahead, behind = (zy * 4 + (x + 1) % 4) * 2, (zy * 4 + (x + 3) % 4) * 2
+    next_line, last_line = ((zy + 1) % 16 * 4 + 2) * 2 + 1, ((zy + 15) % 16 * 4 + 3) * 2 + 1
+    first_relay = jnp.where(x == 3, next_line, behind + 1)
+    starts = (core == 1) & (me < devices - 1)
+    relays = (core == 1) & ((x != 2) | (zy > 0))
+    relays_on = (core == 1) & ((x != 1) | (zy > 0))
+
+    greet(following)
+    greet(preceding)
 
     @pl.when(even)
     def _():
         for step in range(1, 4):
             greet(other_x(step))
+        greet(ahead + 1)
+
+    @pl.when(even & (x > 0))
+    def _():
         for step in range(1, 16):
             greet(other_plane(step))
 
+    @pl.when(core == 1)
+    def _():
+        greet(ahead + 1)
+        greet(behind + 1)
+        greet(behind)
+
+    @pl.when((core == 1) & (x == 3))
+    def _():
+        greet(next_line)
+
+    @pl.when((core == 1) & (x == 2))
+    def _():
+        greet(last_line)
+
     make_weights(w_ref)
-    loads[0].wait()
     totals = index_maps(keep_ref, keepi_ref, keepf_ref, src_ref, rank_ref, places_ref, moves_ref)
     places = pltpu.make_async_copy(places_ref, at, local_sem.at[5])
     places.start()
 
-    @pl.when(me == 0)
-    def _():
-        pl.semaphore_wait(barrier, 19)
-
-    @pl.when((me > 0) & even)
-    def _():
-        pl.semaphore_wait(barrier, 20)
-
-    @pl.when((core == 1) & (me < devices - 1))
-    def _():
-        pl.semaphore_wait(barrier, 2)
-
-    @pl.when(me == devices - 1)
-    def _():
-        pl.semaphore_wait(barrier, 1)
-
-    def tail_copy(s):
+    def everyone_is_here():
+        @pl.when(even & (x == 0))
+        def _():
+            pl.semaphore_wait(barrier, 6)
+
+        @pl.when(even & (x > 0))
+        def _():
+            pl.semaphore_wait(barrier, 21)
+
+        @pl.when((core == 1) & (x < 2))
+        def _():
+            pl.semaphore_wait(barrier, 5)
+
+        @pl.when((core == 1) & (x >= 2))
+        def _():
+            pl.semaphore_wait(barrier, 6)
+
+    def whole_copy(s):
         return remote(
             tail.at[s], windows[s].at[pl.ds(0, SPAN // W)], tail_send.at[s], tail_recv.at[s], following
         )
 
-    lane = lanes_of((8, W))
-    message = jnp.zeros((8, W), F32)
+    def part_copy(s):
+        part = pl.ds(0, COLS - 8 * len(BACK[s]))
+        return remote(
+            tail.at[s, :, part], windows[s].at[pl.ds(0, SPAN // W), part],
+            tail_send.at[s], tail_recv.at[s], following,
+        )
+
+    def hop(unit, k):
+        s, group = UNITS[unit]
+        part = pl.ds(8 * group, 8)
+        src = tail.at[s, :, part] if k == 0 else relay.at[k - 1, unit]
+        dst = windows[s].at[pl.ds(0, SPAN // W), part] if k == 2 else relay.at[k, unit]
+        device = (first_relay, behind + 1, behind)[k]
+        return remote(src, dst, hop_send.at[k, unit], hop_recv.at[k, unit], device)
+
+    def pass_on(unit, k):
+        @pl.when((relays, relays_on)[k - 1])
+        def _():
+            hop(unit, k - 1).wait_recv()
+            hop(unit, k).start()
+
+    def across_copy(k):
+        return remote(across.at[0], across.at[k], scan_send.at[k], across_sem.at[k], other_x(k))
+
+    def plane_copy(k):
+        return remote(plane.at[0], plane.at[k], scan_send.at[3 + k], plane_sem.at[k], other_plane(k))
+
+    up = remote(mine, half, scan_send.at[0], half_sem, preceding)
+    back = remote(send, result, scan_send.at[0], back_sem, following)
+    lines_copy = remote(given, result, scan_send.at[19], given_sem, behind)
+
+    def scan_step(step):
+        if step == 0:
+            mine[...] = take_message(events, keepf_ref, totals)
+
+            @pl.when(core == 1)
+            def _():
+                up.start()
+
+        if step == 1:
+
+            @pl.when(even)
+            def _():
+                up.wait_recv()
+                across[0] = mine[...] + half[...]
+                for k in range(1, 4):
+                    across_copy(k).start()
+
+        if step == 2:
+
+            @pl.when(even & (x > 0))
+            def _():
+                group = across[0]
+                before = jnp.zeros((8, W), F32)
+                for k in range(1, 4):
+                    across_copy(k).wait_recv()
+                    piece = across[k]
+                    group = group + piece
+                    before = before + jnp.where((x + 4 - k) % 4 < x, piece, 0.0)
+                inside[...] = before
+                plane[0] = group
+                for k in range(1, 16):
+                    plane_copy(k).start()
+
+        if step == 3:
+
+            @pl.when(even & (x > 0))
+            def _():
+                lines = jnp.zeros((8, W), F32)
+                for k in range(1, 16):
+                    plane_copy(k).wait_recv()
+                    lines = lines + jnp.where((zy + 16 - k) % 16 < zy, plane[k], 0.0)
+                given[...] = lines
+                result[...] = inside[...] + lines
+
+            @pl.when(even & (x == 1))
+            def _():
+                lines_copy.start()
+
+            @pl.when(even & (x == 0))
+            def _():
+                for k in range(1, 4):
+                    across_copy(k).wait_recv()
+                lines_copy.wait_recv()
+
+            @pl.when(even)
+            def _():
+                send[...] = result[...] + mine[...]
+                back.start()
+
+            @pl.when(core == 1)
+            def _():
+                back.wait_recv()
+
     for s in range(STREAMS):
-        loads[1 + s].wait()
+        if s == 0:
+            loads[1].wait()
         total = prefixes(s, events.at[s], keepf_ref, w_ref, prefix_ref.at[s], exclusive)
+        for unit, k in RELAYS_MIDDLE[s]:
+            pass_on(unit, k)
         compact(s, src_ref, moves_ref, exclusive, table)
         take_tail(table, total, tail.at[s])
-
-        @pl.when(me < devices - 1)
-        def _():
-            tail_copy(s).start()
-
         if s == 0:
+            everyone_is_here()
+
+        @pl.when(even)
+        def _():
+            whole_copy(s).start()
+
+        @pl.when(starts)
+        def _():
+            part_copy(s).start()
+            for unit in range(len(UNITS)):
+                if UNITS[unit][0] == s:
+                    hop(unit, 0).start()
+
+        if s == 0:
+            for load in loads[2:]:
+                load.wait()
             places.wait()
+        for unit, k in RELAYS[s]:
+            pass_on(unit, k)
+        if s < 3:
+            scan_step(s)
         take_early(s, at, table, windows[s])
-        for g in range(4):
-            message = jnp.where(lane == g * 4 + s, total[g * 8 : (g + 1) * 8, :], message)
-        message = jnp.where(lane == 16 + s, totals[s : s + 1, :], message)
-    mine[...] = message
-
-    @pl.when(core == 1)
-    def _():
-        up = remote(mine, half, scan_send.at[0], half_sem, me - 1)
-        up.start()
-        up.wait_send()
-        remote(send, result, scan_send.at[0], back_sem, me - 1).wait_recv()
-
-    @pl.when(even)
-    def _():
-        remote(mine, half, scan_send.at[0], half_sem, me + 1).wait_recv()
-        both = mine[...] + half[...]
-        across[0] = both
-        rows = [
-            remote(across.at[0], across.at[k], scan_send.at[k], across_sem.at[k], other_x(k))
-            for k in range(1, 4)
-        ]
-        for c in rows:
-            c.start()
-        group = both
-        before = jnp.zeros((8, W), F32)
-        for k in range(1, 4):
-            rows[k - 1].wait_recv()
-            piece = across[k]
-            group = group + piece
-            before = before + jnp.where((x + 4 - k) % 4 < x, piece, 0.0)
-        plane[0] = group
-        far = [
-            remote(plane.at[0], plane.at[k], scan_send.at[3 + k], plane_sem.at[k], other_plane(k))
-            for k in range(1, 16)
-        ]
-        for c in far:
-            c.start()
-        for k in range(1, 16):
-            far[k - 1].wait_recv()
-            before = before + jnp.where((zy + 16 - k) % 16 < zy, plane[k], 0.0)
-        result[...] = before
-        send[...] = before + mine[...]
-        back = remote(send, result, scan_send.at[0], back_sem, me + 1)
-        back.start()
-        for c in rows + far:
-            c.wait_send()
-        back.wait_send()
+    scan_step(3)
 
     notes = result[...]
 
@@ -350,18 +465,66 @@
             for t in range(SPAN // W):
                 windows[s][t] = jnp.zeros((COLS, W), F32)
 
+    for s in ORDER:
+
+        @pl.when(core == 1)
+        def _():
+            whole_copy(s).wait_recv()
+
+        @pl.when(even & (me > 0))
+        def _():
+            part_copy(s).wait_recv()
+            for unit in range(len(UNITS)):
+                if UNITS[unit][0] == s:
+                    hop(unit, 2).wait_recv()
+
+        finish(s, at, notes, rank_ref, prefix_ref.at[s], windows[s], mean_ref.at[s], deviation_ref.at[s])
+
+    @pl.when(even)
+    def _():
+        for s in range(STREAMS):
+            whole_copy(s).wait_send()
+        for k in range(1, 4):
+            across_copy(k).wait_send()
+        back.wait_send()
+
+    @pl.when(core == 1)
+    def _():
+        up.wait_send()
+
+    @pl.when(even & (x > 0))
+    def _():
+        for k in range(1, 16):
+            plane_copy(k).wait_send()
+
+    @pl.when(even & (x == 1))
+    def _():
+        lines_copy.wait_send()
+
+    @pl.when(starts)
+    def _():
+        for s in range(STREAMS):
+            part_copy(s).wait_send()
+        for unit in range(len(UNITS)):
+            hop(unit, 0).wait_send()
+
+    for k, sender in ((1, relays), (2, relays_on)):
+
+        @pl.when(sender)
+        def _():
+            for unit in range(len(UNITS)):
+                hop(unit, k).wait_send()
+
+
+def write_kernel(mean_ref, deviation_ref, mean_hbm, deviation_hbm, sems):
+    copies = []
     for s in range(STREAMS):
-
-        @pl.when(me > 0)
-        def _():
-            tail_copy(s).wait_recv()
-
-        finish(s, at, notes, rank_ref, prefix_ref.at[s], windows[s], mean_ref.at[s], deviation_ref.at[s])
-
-    @pl.when(me < devices - 1)
-    def _():
-        for s in range(STREAMS):
-            tail_copy(s).wait_send()
+        copies.append(pltpu.make_async_copy(mean_ref.at[s], mean_hbm.at[s], sems.at[2 * s]))
+        copies.append(pltpu.make_async_copy(deviation_ref.at[s], deviation_hbm.at[s], sems.at[2 * s + 1]))
+    for copy in copies:
+        copy.start()
+    for copy in copies:
+        copy.wait()
 
 
 def per_device(events, keep):
@@ -370,13 +533,12 @@
     dma = pltpu.SemaphoreType.DMA
     hbm = pl.BlockSpec(memory_space=pltpu.HBM)
     vmem = pl.BlockSpec(memory_space=pltpu.VMEM)
-    return pl.pallas_call(
+    mean, deviation = pl.pallas_call(
         kernel,
-        in_specs=[hbm, hbm],
+        in_specs=[vmem, hbm],
         out_specs=[vmem, vmem],
         out_shape=[out, out],
         scratch_shapes=[
-            pltpu.VMEM((STREAMS, ROWS), I32),
             pltpu.VMEM((STREAMS, COLS, ROWS), F32),
             pltpu.VMEM((2 * W, 2 * W), BF16),
             pltpu.VMEM((N, W), I32),
@@ -393,14 +555,25 @@
         ]
         + [pltpu.VMEM((TILES + 3, COLS, W), F32)] * STREAMS
         + [
-            tile, tile, pltpu.VMEM((4, 8, W), F32), pltpu.VMEM((16, 8, W), F32), tile, tile,
-            dma((6,)), dma((STREAMS,)), dma((STREAMS,)), dma, dma((4,)), dma((16,)), dma, dma((19,)),
+            pltpu.VMEM((2, len(UNITS), SPAN // W, 8, W), F32),
+            tile, tile, pltpu.VMEM((4, 8, W), F32), pltpu.VMEM((16, 8, W), F32), tile, tile, tile, tile,
+            dma((6,)), dma((STREAMS,)), dma((STREAMS,)), dma, dma((4,)), dma((16,)), dma, dma, dma((20,)),
+            dma((3, len(UNITS))), dma((3, len(UNITS))),
         ],
         compiler_params=pltpu.CompilerParams(
             collective_id=0, has_side_effects=True, vmem_limit_bytes=44 * 2**20
         ),
         name="windows",
     )(keep, events)
+    return pl.pallas_call(
+        write_kernel,
+        in_specs=[vmem, vmem],
+        out_specs=[hbm, hbm],
+        out_shape=[out, out],
+        scratch_shapes=[dma((2 * STREAMS,))],
+        compiler_params=pltpu.CompilerParams(vmem_limit_bytes=2**20),
+        name="write",
+    )(mean, deviation)
 
 
 def solution(mesh):

time: 49.6 us -> 35.3 us (0.71)
  the two profiles are of different devices: /device:TPU:1 before, /device:TPU:96 now
where the time goes in v2:
time: 35.3 us; the launch traced here: 35.2 us
  Pallas kernels  33.6 us (95%)
  local copies, waits for them, and re-layouts  0.9 us (3%)
  between operations  0.65 us (2%)
    pallas_call x1, Pallas kernels, per_device(): pl.pallas_call(kernel, in_specs=[vmem, hbm], out_specs=[vmem, vmem], out_...  30.3 us
    pallas_call x1, Pallas kernels, per_device(): pl.pallas_call(write_kernel, in_specs=[vmem, vmem], out_specs=[hbm, hbm],...  3.37 us
    unnamed x2, local copies, waits for them, and re-layouts  0.9 us

profile of v2, /device:TPU:96, one launch (start us, length us, event | category | flops | bytes accessed | tf_op | source)
XLA Modules:
  0.0 35.2 jit_solution(18135181328674130387)
XLA Ops:
  0.6 0.0 copy-start
  0.6 0.9 %copy-done = s32[4,8192]{1,0:T(4,128)S(1)} copy-done((s32[4,8192]{1,0:T(4,128)S(1)}, s32[4,8192]{1,0:T(4,128)}, u32[]{:S(2)}) %copy-start) | copy-done | bytes 131096
  1.5 30.3 %windows.1 = (f32[4,32,8192]{2,1,0:T(8,128)S(1)}, f32[4,32,8192]{2,1,0:T(8,128)S(1)}) custom-call(s32[4,8192]{1,0:T(4,128)S(1)} %copy-done, f32[4,32,8192]{2,1,0:T(8,128)} %events_hbm.1), custom_call_target="tpu_custom_call" | custom-call | tf_op jit(solution)/shard_map/windows/pallas_call | solution.py:536
  31.8 3.4 %write.1 = (f32[4,32,8192]{2,1,0:T(8,128)}, f32[4,32,8192]{2,1,0:T(8,128)}) custom-call(f32[4,32,8192]{2,1,0:T(8,128)S(1)} %get-tuple-element.4.mean_ref, f32[4,32,8192]{2,1,0:T(8,128)S(1)} %get-tuple-element.5.deviation_ref), custom_call_target="tpu_custom_call" | custom-call | tf_op jit(solution)/shard_map/write/pallas_call | solution.py:568
Async XLA Ops:
  0.6 0.9 %copy-start = (s32[4,8192]{1,0:T(4,128)S(1)}, s32[4,8192]{1,0:T(4,128)}, u32[]{:S(2)}) copy-start(s32[4,8192]{1,0:T(4,128)} %keep_ref.1) | copy-start | bytes 393220

commit v3 on v2

--- a/solution.py
+++ b/solution.py
@@ -15,11 +15,13 @@
 TABLE = TILES + LEAD + 2
 EARLY = SPAN + W
 N = TILES * STREAMS
-UNITS = ((0, 3), (0, 2), (1, 3), (1, 2))
-BACK = [[g for t, g in UNITS if t == s] for s in range(STREAMS)]
-RELAYS_MIDDLE = ((), (), ((1, 1),), ((2, 1), (1, 2)))
-RELAYS = ((), ((0, 1),), ((0, 2),), ((3, 1), (2, 2), (3, 2)))
-ORDER = (2, 0, 1, 3)
+BASE = ((0, 3), (1, 3), (2, 3))
+EXTRA = ((0, 2), (1, 2))
+UNITS = BASE + EXTRA
+RELAYS_MIDDLE = ((), (), ((0, 1), (3, 1)), ((1, 1), (4, 1)))
+RELAYS_FIRST = ((), (), (), ((0, 2),))
+RELAYS = ((), (), (), ((3, 2), (2, 1), (1, 2), (4, 2), (2, 2)))
+ORDER = (0, 1, 2)
 MESH = pl.DeviceIdType.MESH
 F32 = jnp.float32
 I32 = jnp.int32
@@ -231,14 +233,15 @@
 
 def kernel(
     keep_ref, events_hbm,
-    mean_ref, deviation_ref,
-    events, w_ref, keepi_ref, keepf_ref, src_ref, rank_ref, places_ref, moves_ref, at,
-    prefix_ref, exclusive, table, tail, windows0, windows1, windows2, windows3,
+    mean_ref, deviation_ref, rank_ref, places_ref, prefix3, windows3, notes_ref,
+    events, w_ref, keepi_ref, keepf_ref, src_ref, moves_ref, at,
+    prefix_ref, exclusive, tables, tail, windows0, windows1, windows2,
     relay, mine, half, across, plane, inside, given, send, result,
     local_sem, tail_send, tail_recv, half_sem, across_sem, plane_sem, given_sem, back_sem, scan_send,
     hop_send, hop_recv,
 ):
     windows = (windows0, windows1, windows2, windows3)
+    prefix = [prefix_ref.at[s] for s in range(3)] + [prefix3]
     loads = [None]
     for s in range(STREAMS):
         loads.append(pltpu.make_async_copy(events_hbm.at[s], events.at[s], local_sem.at[1 + s]))
@@ -330,8 +333,11 @@
             tail.at[s], windows[s].at[pl.ds(0, SPAN // W)], tail_send.at[s], tail_recv.at[s], following
         )
 
-    def part_copy(s):
-        part = pl.ds(0, COLS - 8 * len(BACK[s]))
+    def units_of(s, extra):
+        return [u for u in range(len(UNITS)) if UNITS[u][0] == s and (extra or u < len(BASE))]
+
+    def part_copy(s, extra):
+        part = pl.ds(0, COLS - 8 * len(units_of(s, extra)))
         return remote(
             tail.at[s, :, part], windows[s].at[pl.ds(0, SPAN // W), part],
             tail_send.at[s], tail_recv.at[s], following,
@@ -346,7 +352,11 @@
         return remote(src, dst, hop_send.at[k, unit], hop_recv.at[k, unit], device)
 
     def pass_on(unit, k):
-        @pl.when((relays, relays_on)[k - 1])
+        here = (relays, relays_on)[k - 1]
+        if unit >= len(BASE):
+            here = here & (x == 3 - k)
+
+        @pl.when(here)
         def _():
             hop(unit, k - 1).wait_recv()
             hop(unit, k).start()
@@ -409,14 +419,18 @@
             def _():
                 lines_copy.start()
 
+            @pl.when(even & (x > 0))
+            def _():
+                send[...] = result[...] + mine[...]
+                back.start()
+
+        if step == 4:
+
             @pl.when(even & (x == 0))
             def _():
                 for k in range(1, 4):
                     across_copy(k).wait_recv()
                 lines_copy.wait_recv()
-
-            @pl.when(even)
-            def _():
                 send[...] = result[...] + mine[...]
                 back.start()
 
@@ -425,38 +439,48 @@
                 back.wait_recv()
 
     for s in range(STREAMS):
+        table = tables.at[s % 2]
         if s == 0:
             loads[1].wait()
-        total = prefixes(s, events.at[s], keepf_ref, w_ref, prefix_ref.at[s], exclusive)
+        total = prefixes(s, events.at[s], keepf_ref, w_ref, prefix[s], exclusive)
         for unit, k in RELAYS_MIDDLE[s]:
             pass_on(unit, k)
+        if s == 1:
+            scan_step(1)
+        if s == 3:
+            scan_step(3)
         compact(s, src_ref, moves_ref, exclusive, table)
         take_tail(table, total, tail.at[s])
         if s == 0:
             everyone_is_here()
+        for unit, k in RELAYS_FIRST[s]:
+            pass_on(unit, k)
 
         @pl.when(even)
         def _():
             whole_copy(s).start()
 
-        @pl.when(starts)
-        def _():
-            part_copy(s).start()
-            for unit in range(len(UNITS)):
-                if UNITS[unit][0] == s:
+        for extra in (False, True):
+
+            @pl.when(starts & ((x == 3) == extra))
+            def _():
+                part_copy(s, extra).start()
+                for unit in units_of(s, extra):
                     hop(unit, 0).start()
 
         if s == 0:
             for load in loads[2:]:
                 load.wait()
             places.wait()
+            scan_step(0)
+        if s == 1:
+            scan_step(2)
+        if s > 0:
+            take_early(s - 1, at, tables.at[(s - 1) % 2], windows[s - 1])
         for unit, k in RELAYS[s]:
             pass_on(unit, k)
-        if s < 3:
-            scan_step(s)
-        take_early(s, at, table, windows[s])
-    scan_step(3)
-
+    take_early(STREAMS - 1, at, tables.at[(STREAMS - 1) % 2], windows[STREAMS - 1])
+    scan_step(4)
     notes = result[...]
 
     @pl.when(me == 0)
@@ -465,20 +489,25 @@
             for t in range(SPAN // W):
                 windows[s][t] = jnp.zeros((COLS, W), F32)
 
+    notes_ref[...] = notes
+
+    def wait_tail(s):
+        @pl.when(core == 1)
+        def _():
+            whole_copy(s).wait_recv()
+
+        for extra in (False, True):
+
+            @pl.when(even & (me > 0) & ((x == 0) == extra))
+            def _():
+                part_copy(s, extra).wait_recv()
+                for unit in units_of(s, extra):
+                    hop(unit, 2).wait_recv()
+
     for s in ORDER:
-
-        @pl.when(core == 1)
-        def _():
-            whole_copy(s).wait_recv()
-
-        @pl.when(even & (me > 0))
-        def _():
-            part_copy(s).wait_recv()
-            for unit in range(len(UNITS)):
-                if UNITS[unit][0] == s:
-                    hop(unit, 2).wait_recv()
-
-        finish(s, at, notes, rank_ref, prefix_ref.at[s], windows[s], mean_ref.at[s], deviation_ref.at[s])
+        wait_tail(s)
+        finish(s, at, notes, rank_ref, prefix[s], windows[s], mean_ref.at[s], deviation_ref.at[s])
+    wait_tail(3)
 
     @pl.when(even)
     def _():
@@ -501,27 +530,46 @@
     def _():
         lines_copy.wait_send()
 
-    @pl.when(starts)
-    def _():
-        for s in range(STREAMS):
-            part_copy(s).wait_send()
-        for unit in range(len(UNITS)):
-            hop(unit, 0).wait_send()
+    for extra in (False, True):
+
+        @pl.when(starts & ((x == 3) == extra))
+        def _():
+            for s in range(STREAMS):
+                part_copy(s, extra).wait_send()
+                for unit in units_of(s, extra):
+                    hop(unit, 0).wait_send()
 
     for k, sender in ((1, relays), (2, relays_on)):
 
         @pl.when(sender)
         def _():
-            for unit in range(len(UNITS)):
+            for unit in range(len(BASE)):
                 hop(unit, k).wait_send()
 
-
-def write_kernel(mean_ref, deviation_ref, mean_hbm, deviation_hbm, sems):
+        @pl.when(sender & (x == 3 - k))
+        def _():
+            for unit in range(len(BASE), len(UNITS)):
+                hop(unit, k).wait_send()
+
+
+def write_kernel(
+    mean_ref, deviation_ref, rank_ref, places_ref, prefix_ref, windows, notes_ref,
+    mean_hbm, deviation_hbm,
+    mean, deviation, at, sems,
+):
+    places = pltpu.make_async_copy(places_ref, at, sems.at[0])
+    places.start()
     copies = []
-    for s in range(STREAMS):
-        copies.append(pltpu.make_async_copy(mean_ref.at[s], mean_hbm.at[s], sems.at[2 * s]))
-        copies.append(pltpu.make_async_copy(deviation_ref.at[s], deviation_hbm.at[s], sems.at[2 * s + 1]))
+    for s in range(3):
+        copies.append(pltpu.make_async_copy(mean_ref.at[s], mean_hbm.at[s], sems.at[2 * s + 1]))
+        copies.append(pltpu.make_async_copy(deviation_ref.at[s], deviation_hbm.at[s], sems.at[2 * s + 2]))
     for copy in copies:
+        copy.start()
+    places.wait()
+    finish(3, at, notes_ref[...], rank_ref, prefix_ref, windows, mean, deviation)
+    copies.append(pltpu.make_async_copy(mean, mean_hbm.at[3], sems.at[7]))
+    copies.append(pltpu.make_async_copy(deviation, deviation_hbm.at[3], sems.at[8]))
+    for copy in copies[-2:]:
         copy.start()
     for copy in copies:
         copy.wait()
@@ -533,27 +581,34 @@
     dma = pltpu.SemaphoreType.DMA
     hbm = pl.BlockSpec(memory_space=pltpu.HBM)
     vmem = pl.BlockSpec(memory_space=pltpu.VMEM)
-    mean, deviation = pl.pallas_call(
+    three = jax.ShapeDtypeStruct((3, COLS, ROWS), F32)
+    state = [
+        three, three,
+        jax.ShapeDtypeStruct((N, W), I32),
+        jax.ShapeDtypeStruct((8, N), I32),
+        jax.ShapeDtypeStruct((TILES, COLS, W), F32),
+        jax.ShapeDtypeStruct((TILES + 3, COLS, W), F32),
+        jax.ShapeDtypeStruct((8, W), F32),
+    ]
+    state = pl.pallas_call(
         kernel,
         in_specs=[vmem, hbm],
-        out_specs=[vmem, vmem],
-        out_shape=[out, out],
+        out_specs=[vmem] * len(state),
+        out_shape=state,
         scratch_shapes=[
             pltpu.VMEM((STREAMS, COLS, ROWS), F32),
             pltpu.VMEM((2 * W, 2 * W), BF16),
             pltpu.VMEM((N, W), I32),
             pltpu.VMEM((N, W), F32),
             pltpu.VMEM((N, W), I32),
-            pltpu.VMEM((N, W), I32),
-            pltpu.VMEM((8, N), I32),
             pltpu.VMEM((6, N + STREAMS * LEAD, W), I32),
             pltpu.SMEM((8, N), I32),
-            pltpu.VMEM((STREAMS, TILES, COLS, W), F32),
+            pltpu.VMEM((3, TILES, COLS, W), F32),
             pltpu.VMEM((TILES, COLS, W), F32),
-            pltpu.VMEM((TABLE, COLS, W), F32),
+            pltpu.VMEM((2, TABLE, COLS, W), F32),
             pltpu.VMEM((STREAMS, SPAN // W, COLS, W), F32),
         ]
-        + [pltpu.VMEM((TILES + 3, COLS, W), F32)] * STREAMS
+        + [pltpu.VMEM((TILES + 3, COLS, W), F32)] * 3
         + [
             pltpu.VMEM((2, len(UNITS), SPAN // W, 8, W), F32),
             tile, tile, pltpu.VMEM((4, 8, W), F32), pltpu.VMEM((16, 8, W), F32), tile, tile, tile, tile,
@@ -561,19 +616,21 @@
             dma((3, len(UNITS))), dma((3, len(UNITS))),
         ],
         compiler_params=pltpu.CompilerParams(
-            collective_id=0, has_side_effects=True, vmem_limit_bytes=44 * 2**20
+            collective_id=0, has_side_effects=True, vmem_limit_bytes=43 * 2**20
         ),
         name="windows",
     )(keep, events)
     return pl.pallas_call(
         write_kernel,
-        in_specs=[vmem, vmem],
+        in_specs=[vmem] * len(state),
         out_specs=[hbm, hbm],
         out_shape=[out, out],
-        scratch_shapes=[dma((2 * STREAMS,))],
-        compiler_params=pltpu.CompilerParams(vmem_limit_bytes=2**20),
+        scratch_shapes=[
+            pltpu.VMEM((COLS, ROWS), F32), pltpu.VMEM((COLS, ROWS), F32), pltpu.SMEM((8, N), I32), dma((9,)),
+        ],
+        compiler_params=pltpu.CompilerParams(vmem_limit_bytes=4 * 2**20),
         name="write",
-    )(mean, deviation)
+    )(*state)
 
 
 def solution(mesh):

time: 35.3 us -> 32.9 us (0.932)
  Pallas kernels: 33.6 us -> 31.2 us
    pallas_call x2, Pallas kernels: 33.6 us -> 31.2 us  [the longest x1 27.8 us: per_device(): pl.pallas_call(kernel, in_specs=[vmem, hbm], out_specs=[vmem] * len(state...]
where the time goes in v3:
time: 32.9 us; the launch traced here: 32.8 us
  Pallas kernels  31.2 us (95%)
  local copies, waits for them, and re-layouts  0.9 us (3%)
  between operations  0.65 us (2%)
    pallas_call x1, Pallas kernels, per_device(): pl.pallas_call(kernel, in_specs=[vmem, hbm], out_specs=[vmem] * len(state...  27.8 us
    pallas_call x1, Pallas kernels, per_device(): pl.pallas_call(write_kernel, in_specs=[vmem] * len(state), out_specs=[hbm...  3.38 us
    unnamed x2, local copies, waits for them, and re-layouts  0.9 us

profile of v3, /device:TPU:96, one launch (start us, length us, event | category | flops | bytes accessed | tf_op | source)
XLA Modules:
  0.0 32.8 jit_solution(18001789396405440673)
XLA Ops:
  0.6 0.0 copy-start
  0.6 0.9 %copy-done = s32[4,8192]{1,0:T(4,128)S(1)} copy-done((s32[4,8192]{1,0:T(4,128)S(1)}, s32[4,8192]{1,0:T(4,128)}, u32[]{:S(2)}) %copy-start) | copy-done | bytes 131096
  1.5 27.8 %windows.1 = (f32[3,32,8192]{2,1,0:T(8,128)S(1)}, f32[3,32,8192]{2,1,0:T(8,128)S(1)}, s32[256,128]{1,0:T(8,128)S(1)}, s32[8,256]{1,0:T(8,128)S(1)}, f32[64,32,12...) custom-call(s32[4,8192]{1,0:T(4,128)S(1)} %copy-done, f32[4,32,8192]{2,1,0:T(8,128)} %events_hbm.1), custom_call_target="tpu_custom_call" | custom-call | tf_op jit(solution)/shard_map/windows/pallas_call | solution.py:593
  29.4 3.4 %write.1 = (f32[4,32,8192]{2,1,0:T(8,128)}, f32[4,32,8192]{2,1,0:T(8,128)}) custom-call(f32[3,32,8192]{2,1,0:T(8,128)S(1)} %get-tuple-element.9.mean_ref, f32[3,32,8192]{2,1,0:T(8,128)S(1)} %get-tuple-element.10.deviation_ref, s32[256,128]{1,0:T(8,128)S(1)} %get-tuple-element.11.rank_ref, s32[8,256]{1,0:T(8,128)S(1)} %get-tuple-element.12.places_ref, ...), custom_call_target="tpu_custom_call" | custom-call | tf_op jit(solution)/shard_map/write/pallas_call | solution.py:623
Async XLA Ops:
  0.6 0.9 %copy-start = (s32[4,8192]{1,0:T(4,128)S(1)}, s32[4,8192]{1,0:T(4,128)}, u32[]{:S(2)}) copy-start(s32[4,8192]{1,0:T(4,128)} %keep_ref.1) | copy-start | bytes 393220

commit v4 on v3

--- a/solution.py
+++ b/solution.py
@@ -244,7 +244,7 @@
     prefix = [prefix_ref.at[s] for s in range(3)] + [prefix3]
     loads = [None]
     for s in range(STREAMS):
-        loads.append(pltpu.make_async_copy(events_hbm.at[s], events.at[s], local_sem.at[1 + s]))
+        loads.append(pltpu.make_async_copy(events_hbm.at[s], events.at[s, :, pl.ds(0, ROWS)], local_sem.at[1 + s]))
     for load in loads[1:]:
         load.start()
     devices = lax.axis_size("rows")
@@ -596,7 +596,7 @@
         out_specs=[vmem] * len(state),
         out_shape=state,
         scratch_shapes=[
-            pltpu.VMEM((STREAMS, COLS, ROWS), F32),
+            pltpu.VMEM((STREAMS, COLS, ROWS + W), F32),
             pltpu.VMEM((2 * W, 2 * W), BF16),
             pltpu.VMEM((N, W), I32),
             pltpu.VMEM((N, W), F32),

time: 32.9 us -> 32.9 us (level)
  no operation moved by 1% of the time
where the time goes in v4:
time: 32.9 us; the launch traced here: 32.8 us
  Pallas kernels  31.3 us (95%)
  local copies, waits for them, and re-layouts  0.9 us (3%)
  between operations  0.65 us (2%)
    pallas_call x1, Pallas kernels, per_device(): pl.pallas_call(kernel, in_specs=[vmem, hbm], out_specs=[vmem] * len(state...  27.9 us
    pallas_call x1, Pallas kernels, per_device(): pl.pallas_call(write_kernel, in_specs=[vmem] * len(state), out_specs=[hbm...  3.38 us
    unnamed x2, local copies, waits for them, and re-layouts  0.9 us

profile of v4, /device:TPU:96, one launch (start us, length us, event | category | flops | bytes accessed | tf_op | source)
XLA Modules:
  0.0 32.8 jit_solution(13146276016208205082)
XLA Ops:
  0.6 0.0 copy-start
  0.6 0.9 %copy-done = s32[4,8192]{1,0:T(4,128)S(1)} copy-done((s32[4,8192]{1,0:T(4,128)S(1)}, s32[4,8192]{1,0:T(4,128)}, u32[]{:S(2)}) %copy-start) | copy-done | bytes 131096
  1.5 27.9 %windows.1 = (f32[3,32,8192]{2,1,0:T(8,128)S(1)}, f32[3,32,8192]{2,1,0:T(8,128)S(1)}, s32[256,128]{1,0:T(8,128)S(1)}, s32[8,256]{1,0:T(8,128)S(1)}, f32[64,32,12...) custom-call(s32[4,8192]{1,0:T(4,128)S(1)} %copy-done, f32[4,32,8192]{2,1,0:T(8,128)} %events_hbm.1), custom_call_target="tpu_custom_call" | custom-call | tf_op jit(solution)/shard_map/windows/pallas_call | solution.py:593
  29.4 3.4 %write.1 = (f32[4,32,8192]{2,1,0:T(8,128)}, f32[4,32,8192]{2,1,0:T(8,128)}) custom-call(f32[3,32,8192]{2,1,0:T(8,128)S(1)} %get-tuple-element.9.mean_ref, f32[3,32,8192]{2,1,0:T(8,128)S(1)} %get-tuple-element.10.deviation_ref, s32[256,128]{1,0:T(8,128)S(1)} %get-tuple-element.11.rank_ref, s32[8,256]{1,0:T(8,128)S(1)} %get-tuple-element.12.places_ref, ...), custom_call_target="tpu_custom_call" | custom-call | tf_op jit(solution)/shard_map/write/pallas_call | solution.py:623
Async XLA Ops:
  0.6 0.9 %copy-start = (s32[4,8192]{1,0:T(4,128)S(1)}, s32[4,8192]{1,0:T(4,128)}, u32[]{:S(2)}) copy-start(s32[4,8192]{1,0:T(4,128)} %keep_ref.1) | copy-start | bytes 393220
